TPU v7x, 32 devices: a whole 2x2x4 slice. The times are simulated.
32 devices in a mesh: rows: 16 (over z, y, x), cols: 2 (over core).
Axes of the slice: x: 2, y: 2, z: 4, core: 2. Of those that a mesh axis runs over, the one named last changes fastest.
Arguments:
- rhs: float32 [2, 96, 6144], P('cols', 'rows'), may hold values from -6 to 6
- pattern: int32 [48, 2], P(None, 'cols'), may hold values 0 or 1
- front_blocks: int32 [16, 4], replicated, may hold values from 0 to 47, as said below
- front_slot: int32 [16], replicated, may hold values from 0 to 31, as said below
- pivot_inverse: float32 [32, 256, 256], P('rows'), may hold values from -0.375 to 0.375
- update_factor: float32 [32, 256, 256], P('rows'), may hold values from -0.375 to 0.375
Outputs:
- solution: float32 [2, 96, 6144], P('cols', 'rows')
Inputs may be any that keep to these rules, and one draw needn't show every extreme that they name: `front_blocks`: columns 0 and 1 together name every row block that is no contribution block exactly once; columns 2 and 3 of a front are two different blocks, never a pivot block of any front. `front_slot`: all different; slot s belongs to index s // 2 of rows; some index holds 2 fronts in every draw; slots that no front names are unused.
All inputs are finite; a program needn't handle non-finite values. No bound on the sum of `pattern` on one device may be relied on, other than what follows from the above.
Results may differ from a plain program's by a relative error of at most 0.0001.
Values sent between devices are 32-bit elements; how exact they have to be, the bound alone decides.
A program may use at most 64 MiB of HBM per device.

v0:
```python
import jax
import jax.numpy as jnp
from jax import lax
from jax.sharding import PartitionSpec as P

BLOCK = 128
PIV = 256


def solve_slots(arrived, inverse_part, factor_part):
    width = inverse_part.shape[1]
    strict_lower = jnp.tril(jnp.ones((width, width), jnp.float32), -1)
    inverse = jnp.eye(width, dtype=jnp.float32)[None] + strict_lower[None] * inverse_part
    solved = jnp.einsum("kcj,kij->kci", arrived, inverse, precision=lax.Precision.HIGHEST)
    update = jnp.einsum("kcj,kij->kci", solved, factor_part, precision=lax.Precision.HIGHEST)
    return jnp.concatenate([solved, update], axis=2)


def on_device(rhs, pattern, front_blocks, front_slot, pivot_inverse, update_factor):
    fronts = front_blocks.shape[0]
    columns = rhs.shape[1]
    total_rows = rhs.shape[2]
    block_count = total_rows // BLOCK
    slot_dev = pivot_inverse.shape[0]
    devices = lax.axis_size("rows")
    pivot_blocks = front_blocks[:, :2].reshape(-1)
    contrib_blocks = front_blocks[:, 2:].reshape(-1)
    block_mask = pattern[:, 0].astype(jnp.float32)
    masked = rhs[0].reshape(columns, block_count, BLOCK) * block_mask[None, :, None]
    picked = jnp.swapaxes(
        jnp.take(masked, pivot_blocks, axis=1).reshape(columns, fronts, PIV), 0, 1
    )
    outbound = jnp.zeros((slot_dev * devices, columns, PIV), jnp.float32).at[front_slot].set(picked)
    arrived = lax.all_to_all(outbound, "rows", split_axis=0, concat_axis=1, tiled=True)
    worked = solve_slots(arrived, pivot_inverse, update_factor)
    returned = lax.all_to_all(worked, "rows", split_axis=1, concat_axis=0, tiled=True)
    gotten = returned[front_slot]
    solved = jnp.swapaxes(gotten[:, :, :PIV], 0, 1).reshape(columns, 2 * fronts, BLOCK)
    update = jnp.swapaxes(gotten[:, :, PIV:], 0, 1).reshape(columns, 2 * fronts, BLOCK)
    result = masked.at[:, pivot_blocks].set(solved)
    result = result.at[:, contrib_blocks].add(-update)
    return result.reshape(columns, total_rows)[None]


def solution(mesh):
    return jax.shard_map(
        on_device,
        mesh=mesh,
        in_specs=(
            P("cols", "rows", None),
            P(None, "cols"),
            P(),
            P(),
            P("rows", None, None),
            P("rows", None, None),
        ),
        out_specs=P("cols", "rows", None),
        check_vma=False,
    )
```

profile of v0, /device:TPU:0, one launch (start us, length us, event | category | flops | bytes accessed | tf_op | source)
XLA Modules:
  0.0 48.0 jit_solution(16247769093487404575)
XLA Ops:
  0.0 0.0 copy-start
  0.0 0.0 copy-start.2
  0.0 0.8 %fusion.10 = (s32[16,2]{0,1:T(2,128)S(1)}, s32[16,2]{0,1:T(2,128)S(1)}) fusion(s32[16,4]{0,1:T(4,128)} %param.8), kind=kLoop, calls=%fused_computation.31 | loop fusion | bytes 512 | tf_op jit(solution)/shard_map/slice | solution.py:27
  0.8 0.0 copy-done.2
  0.8 0.1 copy.33
  0.9 0.1 reshape.108
  1.0 0.0 copy-start.3
  1.0 0.6 %copy-done.3 = s32[48,1]{0,1:T(1,128)S(1)} copy-done((s32[48,1]{0,1:T(1,128)S(1)}, s32[48,1]{0,1:T(1,128)}, u32[]{:S(2)}) %copy-start.3) | copy-done | bytes 216
  1.7 0.1 copy.34
  1.8 0.1 broadcast_in_dim.35
  1.8 0.0 copy-start.4
  1.9 0.6 %copy-done.4 = s32[16]{0:T(128)S(1)} copy-done((s32[16]{0:T(128)S(1)}, s32[16]{0:T(128)}, u32[]{:S(2)}) %copy-start.4) | copy-done | bytes 88
  2.5 1.0 %copy_multiply_fusion = f32[6,48,128]{2,0,1:T(8,128)S(1)} fusion(f32[6,48,128]{2,1,0:T(8,128)} %bitcast.45, f32[48]{0:T(128)S(1)} %convert_bitcast_fusion), kind=kLoop, calls=%fused_computation.16 | loop fusion | flops 36864 | bytes 295104 | tf_op jit(solution)/shard_map/mul | solution.py:29
  3.5 0.6 %gather_fusion = f32[32,6,128]{2,1,0:T(8,128)S(1)} fusion(f32[6,48,128]{2,0,1:T(8,128)S(1)} %copy_multiply_fusion, s32[1024]{0:T(1024)S(1)} %pad_clamp_fusion.1), kind=kCustom, calls=%fused_computation | custom fusion | bytes 196736 | tf_op jit(solution)/shard_map/jit(_take)/gather | solution.py:31
  4.2 0.7 %broadcast_in_dim.33 = f32[32,6,256]{2,1,0:T(8,128)} broadcast(f32[]{:T(128)} %constant.10.clone.1), dimensions={} | broadcast | bytes 196612 | tf_op jit(solution)/shard_map/broadcast_in_dim | solution.py:33
  4.9 2.2 %scatter_fusion = f32[32,6,256]{2,1,0:T(8,128)} fusion(f32[32,6,256]{2,1,0:T(8,128)} %broadcast_in_dim.33, s32[16]{0:T(128)S(1)} %compare_select_fusion.2, f32[16,6,256]{2,1,0:T(8,128)S(1)} %select_bitcast_fusion), kind=kCustom, calls=%fused_computation.2 | custom fusion | bytes 294976 | tf_op jit(solution)/shard_map/scatter | solution.py:33
  7.1 8.3 %all-to-all-start = ((f32[32,6,256]{2,1,0:T(8,128)}), f32[32,6,256]{2,1,0:T(8,128)S(1)}, u32[]{:S(2)}, u32[]{:S(2)}) async-start(f32[32,6,256]{2,1,0:T(8,128)} %scatter_fusion), calls=%async_computation | async-start | bytes 524288 | tf_op jit(solution)/shard_map/all_to_all | solution.py:34
  15.4 0.0 copy-start.1
  15.5 0.1 fusion.6
  15.6 9.7 %all-to-all-done = f32[32,6,256]{2,1,0:T(8,128)S(1)} async-done(((f32[32,6,256]{2,1,0:T(8,128)}), f32[32,6,256]{2,1,0:T(8,128)S(1)}, u32[]{:S(2)}, u32[]{:S(2)}) %all-to-all-start) | async-done | bytes 196640 | tf_op jit(solution)/shard_map/all_to_all | solution.py:34
  25.3 0.1 copy.35
  25.4 0.0 copy-done.1
  25.4 0.6 %fusion = f32[2,96,256]{2,1,0:T(8,128)S(1)} fusion(f32[2,256,256]{2,1,0:T(8,128)S(1)} %copy-done.1, f32[256,256]{1,0:T(8,128)S(1)} %fusion.6, f32[256,256]{1,0:T(8,128)S(1)} %fusion.5, f32[2,96,256]{2,0,1:T(2,128)S(1)} %bitcast.41), kind=kOutput, calls=%fused_computation.5 | convolution fusion | flops 151257088 | bytes 1441792 | tf_op jit(solution)/shard_map/kcj,kij->kci/dot_general | solution.py:14
  26.1 0.0 copy-done
  26.1 0.6 %fusion.11 = f32[2,96,256]{2,1,0:T(8,128)S(1)} fusion(f32[2,96,256]{2,1,0:T(8,128)S(1)} %fusion, f32[2,256,256]{2,1,0:T(8,128)S(1)} %copy-done), kind=kOutput, calls=%fused_computation.32 | convolution fusion | flops 150994944 | bytes 917504 | tf_op jit(solution)/shard_map/kcj,kij->kci/dot_general | solution.py:15
  26.7 1.1 %copy.37 = f32[2,96,512]{2,0,1:T(2,128)} copy(f32[2,96,512]{2,1,0:T(8,128)S(1)} %pad_maximum_fusion) | data formatting | bytes 786432 | tf_op jit(solution)/shard_map/concatenate | solution.py:16
  27.8 3.6 %all-to-all-start.1 = ((f32[2,96,512]{2,0,1:T(2,128)}), f32[2,96,512]{2,0,1:T(2,128)S(1)}, u32[]{:S(2)}, u32[]{:S(2)}) async-start(f32[2,96,512]{2,0,1:T(2,128)} %copy.37), calls=%async_computation.1 | async-start | bytes 786432 | tf_op jit(solution)/shard_map/all_to_all | solution.py:36
  31.3 0.1 copy.40
  31.4 0.1 reshape.110
  31.5 11.8 %all-to-all-done.1 = f32[2,96,512]{2,0,1:T(2,128)S(1)} async-done(((f32[2,96,512]{2,0,1:T(2,128)}), f32[2,96,512]{2,0,1:T(2,128)S(1)}, u32[]{:S(2)}, u32[]{:S(2)}) %all-to-all-start.1) | async-done | bytes 393248 | tf_op jit(solution)/shard_map/all_to_all | solution.py:36
  43.3 0.1 copy.42
  43.4 0.6 %gather_fusion.1 = f32[16,6,512]{2,1,0:T(8,128)S(1)} fusion(f32[32,6,512]{2,1,0:T(8,128)S(1)} %bitcast.39, s32[1024]{0:T(1024)S(1)} %pad_clamp_fusion), kind=kCustom, calls=%fused_computation.1 | custom fusion | bytes 393280 | tf_op jit(solution)/shard_map/gather | solution.py:37
  44.0 1.5 %scatter_fusion.1 = f32[6,48,128]{2,0,1:T(8,128)S(1)} fusion(f32[6,48,128]{2,0,1:T(8,128)S(1)} %copy_multiply_fusion, s32[32]{0:T(128)S(1)} %fusion.8, f32[32,6,128]{2,1,0:T(8,128)S(1)} %bitcast.44), kind=kCustom, calls=%fused_computation.3 | custom fusion | bytes 295040 | tf_op jit(solution)/shard_map/scatter | solution.py:40
  45.5 1.7 %scatter_fusion.2 = f32[6,48,128]{2,0,1:T(8,128)S(1)} fusion(f32[6,48,128]{2,0,1:T(8,128)S(1)} %scatter_fusion.1, s32[32]{0:T(128)S(1)} %fusion.9, f32[32,6,128]{2,1,0:T(8,128)S(1)} %bitcast.43), kind=kCustom, calls=%fused_computation.4 | custom fusion | flops 24576 | bytes 295040 | tf_op jit(solution)/shard_map/scatter-add | solution.py:41
  47.2 0.8 %copy.41 = f32[1,6,6144]{2,0,1:T(1,128)} copy(f32[1,6,6144]{2,1,0:T(8,128)S(1)} %bitcast.37) | data formatting | bytes 294912 | tf_op jit(solution)/shard_map/broadcast_in_dim;reshape | solution.py:42
  (13 shorter events, 0.1 us)
Async XLA Ops:
  0.0 26.1 %copy-start = (f32[2,256,256]{2,1,0:T(8,128)S(1)}, f32[2,256,256]{2,1,0:T(8,128)}, u32[]{:S(2)}) copy-start(f32[2,256,256]{2,1,0:T(8,128)} %param.11) | copy-start | bytes 1572868
  0.0 0.8 %copy-start.2 = (s32[16,4]{0,1:T(4,128)S(1)}, s32[16,4]{0,1:T(4,128)}, u32[]{:S(2)}) copy-start(s32[16,4]{0,1:T(4,128)} %param.8) | copy-start | bytes 772
  1.0 0.7 %copy-start.3 = (s32[48,1]{0,1:T(1,128)S(1)}, s32[48,1]{0,1:T(1,128)}, u32[]{:S(2)}) copy-start(s32[48,1]{0,1:T(1,128)} %param.7) | copy-start | bytes 580
  1.8 0.7 %copy-start.4 = (s32[16]{0:T(128)S(1)}, s32[16]{0:T(128)}, u32[]{:S(2)}) copy-start(s32[16]{0:T(128)} %param.9) | copy-start | bytes 196
  7.1 18.2 %all-to-all-start = ((f32[32,6,256]{2,1,0:T(8,128)}), f32[32,6,256]{2,1,0:T(8,128)S(1)}, u32[]{:S(2)}, u32[]{:S(2)}) async-start(f32[32,6,256]{2,1,0:T(8,128)} %scatter_fusion), calls=%async_computation | async-start | bytes 524288 | tf_op jit(solution)/shard_map/all_to_all | solution.py:34
  15.4 10.0 %copy-start.1 = (f32[2,256,256]{2,1,0:T(8,128)S(1)}, f32[2,256,256]{2,1,0:T(8,128)}, u32[]{:S(2)}) copy-start(f32[2,256,256]{2,1,0:T(8,128)} %param.10) | copy-start | bytes 1572868
  27.8 15.5 %all-to-all-start.1 = ((f32[2,96,512]{2,0,1:T(2,128)}), f32[2,96,512]{2,0,1:T(2,128)S(1)}, u32[]{:S(2)}, u32[]{:S(2)}) async-start(f32[2,96,512]{2,0,1:T(2,128)} %copy.37), calls=%async_computation.1 | async-start | bytes 786432 | tf_op jit(solution)/shard_map/all_to_all | solution.py:36
where the time goes:
time: 48.4 us; the launch traced here: 48 us
  waiting for transfers between devices  21.5 us (44%)
  starting transfers between devices  11.9 us (25%)
  local copies, waits for them, and re-layouts  10.2 us (21%)
  other arithmetic  2.92 us (6%)
  matrix products  1.25 us (3%)
    all_to_all x1, waiting for transfers between devices, on_device(): lax.all_to_all(worked, 'rows', split_axis=1, concat_axis=0, tiled=True)  11.8 us
    all_to_all x1, waiting for transfers between devices, on_device(): lax.all_to_all(outbound, 'rows', split_axis=0, concat_axis=1, tiled=True)  9.71 us
    all_to_all x1, starting transfers between devices, on_device(): lax.all_to_all(outbound, 'rows', split_axis=0, concat_axis=1, tiled=True)  8.34 us
    all_to_all x1, starting transfers between devices, on_device(): lax.all_to_all(worked, 'rows', split_axis=1, concat_axis=0, tiled=True)  3.56 us
    scatter x1, local copies, waits for them, and re-layouts, on_device(): jnp.zeros((slot_dev * devices, columns, PIV), jnp.float32).at[front_slot]  2.2 us
    scatter-add x1, other arithmetic, on_device(): result = result.at[:, contrib_blocks].add(-update)  1.66 us
    scatter x1, local copies, waits for them, and re-layouts, on_device(): result = masked.at[:, pivot_blocks].set(solved)  1.48 us
    unnamed x11, local copies, waits for them, and re-layouts  1.3 us
  transfers between devices with their start and end apart: 2, of which 2 were waited for; matrix products, arithmetic and copies ran while one was open for 1% of the time, Pallas kernels for 0%

commit v1 on v0

--- a/solution.py
+++ b/solution.py
@@ -1,3 +1,4 @@
+import functools
 import jax
 import jax.numpy as jnp
 from jax import lax
@@ -5,6 +6,22 @@
 
 BLOCK = 128
 PIV = 256
+
+
+def pieces_all_process(here_x, axis_key):
+    aux = jnp.concatenate(
+        lax.all_to_all(
+            jnp.stack(jnp.split(here_x, lax.axis_size(axis_key), axis=0)),
+            axis_name=axis_key,
+            split_axis=0,
+            concat_axis=0,
+        ),
+        axis=1,
+    )
+    return aux
+
+
+trace_copies = functools.partial(pieces_all_process, axis_key="rows")
 
 
 def solve_slots(arrived, inverse_part, factor_part):
@@ -31,7 +48,7 @@
         jnp.take(masked, pivot_blocks, axis=1).reshape(columns, fronts, PIV), 0, 1
     )
     outbound = jnp.zeros((slot_dev * devices, columns, PIV), jnp.float32).at[front_slot].set(picked)
-    arrived = lax.all_to_all(outbound, "rows", split_axis=0, concat_axis=1, tiled=True)
+    arrived = trace_copies(outbound)
     worked = solve_slots(arrived, pivot_inverse, update_factor)
     returned = lax.all_to_all(worked, "rows", split_axis=1, concat_axis=0, tiled=True)
     gotten = returned[front_slot]

time: 48.4 us -> 46.3 us (0.957)
  waiting for transfers between devices: 21.5 us -> 20.3 us
  local copies, waits for them, and re-layouts: 10.2 us -> 9.09 us
    all_to_all x1, waiting for transfers between devices: 9.71 us -> 8.5 us  [pieces_all_process(): lax.all_to_all(jnp.stack(jnp.split(here_x, lax.axis_size(axis_key), axis=...]
    scatter x1, local copies, waits for them, and re-layouts: 2.2 us -> 1.02 us  [on_device(): jnp.zeros((slot_dev * devices, columns, PIV), jnp.float32).at[front_slot]]
    another operation x0 -> x2, local copies, waits for them, and re-layouts: none -> 0.78 us  [pieces_all_process(): jnp.stack(jnp.split(here_x, lax.axis_size(axis_key), axis=0))]
    broadcast_in_dim x1, local copies, waits for them, and re-layouts: 0.71 us -> 0.02 us  [on_device(): jnp.zeros((slot_dev * devices, columns, PIV), jnp.float32).at[front_slot]]
    unnamed x11 -> x26, local copies, waits for them, and re-layouts: 1.3 us -> 1.36 us
where the time goes in v1:
time: 46.3 us; the launch traced here: 45.9 us
  waiting for transfers between devices  20.3 us (44%)
  starting transfers between devices  12 us (26%)
  local copies, waits for them, and re-layouts  9.09 us (20%)
  other arithmetic  2.92 us (6%)
  matrix products  1.25 us (3%)
    all_to_all x1, waiting for transfers between devices, on_device(): lax.all_to_all(worked, 'rows', split_axis=1, concat_axis=0, tiled=True)  11.8 us
    all_to_all x1, waiting for transfers between devices, pieces_all_process(): lax.all_to_all(jnp.stack(jnp.split(here_x, lax.axis_size(axis_key), axis=...  8.5 us
    all_to_all x1, starting transfers between devices, pieces_all_process(): lax.all_to_all(jnp.stack(jnp.split(here_x, lax.axis_size(axis_key), axis=...  8.47 us
    all_to_all x1, starting transfers between devices, on_device(): lax.all_to_all(worked, 'rows', split_axis=1, concat_axis=0, tiled=True)  3.55 us
    scatter-add x1, other arithmetic, on_device(): result = result.at[:, contrib_blocks].add(-update)  1.66 us
    scatter x1, local copies, waits for them, and re-layouts, on_device(): result = masked.at[:, pivot_blocks].set(solved)  1.48 us
    unnamed x26, local copies, waits for them, and re-layouts  1.36 us
    concatenate x1, local copies, waits for them, and re-layouts, solve_slots(): return jnp.concatenate([solved, update], axis=2)  1.05 us
  transfers between devices with their start and end apart: 2, of which 2 were waited for; matrix products, arithmetic and copies ran while one was open for 1% of the time, Pallas kernels for 0%

profile of v1, /device:TPU:0, one launch (start us, length us, event | category | flops | bytes accessed | tf_op | source)
XLA Modules:
  0.0 45.9 jit_solution(15450669834033965355)
XLA Ops:
  0.0 0.0 copy-start
  0.0 0.0 copy-start.2
  0.0 0.8 %fusion.10 = (s32[16,2]{0,1:T(2,128)S(1)}, s32[16,2]{0,1:T(2,128)S(1)}) fusion(s32[16,4]{0,1:T(4,128)} %param.8), kind=kLoop, calls=%fused_computation.63 | loop fusion | bytes 512 | tf_op jit(solution)/shard_map/slice | solution.py:44
  0.8 0.0 copy-done.2
  0.8 0.1 copy.33
  0.9 0.1 reshape.114
  1.0 0.0 copy-start.3
  1.0 0.6 %copy-done.3 = s32[16]{0:T(128)S(1)} copy-done((s32[16]{0:T(128)S(1)}, s32[16]{0:T(128)}, u32[]{:S(2)}) %copy-start.3) | copy-done | bytes 88
  1.6 0.0 copy-start.4
  1.6 0.6 %copy-done.4 = s32[48,1]{0,1:T(1,128)S(1)} copy-done((s32[48,1]{0,1:T(1,128)S(1)}, s32[48,1]{0,1:T(1,128)}, u32[]{:S(2)}) %copy-start.4) | copy-done | bytes 216
  2.3 0.1 copy.34
  2.4 0.1 broadcast_in_dim.35
  2.5 1.0 %copy_multiply_fusion = f32[6,48,128]{2,0,1:T(8,128)S(1)} fusion(f32[6,48,128]{2,1,0:T(8,128)} %bitcast.107, f32[48]{0:T(128)S(1)} %convert_bitcast_fusion), kind=kLoop, calls=%fused_computation.16 | loop fusion | flops 36864 | bytes 295104 | tf_op jit(solution)/shard_map/mul | solution.py:46
  3.5 0.6 %gather_fusion = f32[32,6,128]{2,1,0:T(8,128)S(1)} fusion(f32[6,48,128]{2,0,1:T(8,128)S(1)} %copy_multiply_fusion, s32[1024]{0:T(1024)S(1)} %get-tuple-element.10), kind=kCustom, calls=%fused_computation | custom fusion | bytes 196736 | tf_op jit(solution)/shard_map/jit(_take)/gather | solution.py:48
  4.2 1.0 %scatter_fusion = f32[32,6,256]{2,1,0:T(8,128)S(1)} fusion(f32[32,6,256]{2,1,0:T(8,128)S(1)} %broadcast_in_dim.33, s32[16]{0:T(128)S(1)} %compare_select_fusion.2, f32[16,6,256]{2,1,0:T(8,128)S(1)} %select_bitcast_fusion), kind=kCustom, calls=%fused_computation.2 | custom fusion | bytes 294976 | tf_op jit(solution)/shard_map/scatter | solution.py:50
  5.4 0.8 %copy.35 = f32[16,2,6,256]{3,1,2,0:T(2,128)} copy(f32[16,2,6,256]{3,2,1,0:T(8,128)S(1)} %constant_dynamic-update-slice_fusion) | data formatting | bytes 393216 | tf_op jit(solution)/shard_map/stack | solution.py:14
  6.2 0.0 copy-start.1
  6.2 8.5 %all-to-all-start = ((f32[16,2,6,256]{3,1,2,0:T(2,128)}), f32[16,2,6,256]{3,1,2,0:T(2,128)S(1)}, u32[]{:S(2)}, u32[]{:S(2)}) async-start(f32[16,2,6,256]{3,1,2,0:T(2,128)} %copy.35), calls=%async_computation | async-start | bytes 393216 | tf_op jit(solution)/shard_map/all_to_all | solution.py:13
  14.7 0.1 fusion.6
  14.8 8.5 %all-to-all-done = f32[16,2,6,256]{3,1,2,0:T(2,128)S(1)} async-done(((f32[16,2,6,256]{3,1,2,0:T(2,128)}), f32[16,2,6,256]{3,1,2,0:T(2,128)S(1)}, u32[]{:S(2)}, u32[]{:S(2)}) %all-to-all-start) | async-done | bytes 196640 | tf_op jit(solution)/shard_map/all_to_all | solution.py:13
  23.3 0.0 copy-done.1
  23.3 0.6 %fusion = f32[2,96,256]{2,1,0:T(8,128)S(1)} fusion(f32[2,256,256]{2,1,0:T(8,128)S(1)} %copy-done.1, f32[256,256]{1,0:T(8,128)S(1)} %fusion.6, f32[256,256]{1,0:T(8,128)S(1)} %fusion.5, f32[2,96,256]{2,0,1:T(2,128)S(1)} %bitcast.103), kind=kOutput, calls=%fused_computation.5 | convolution fusion | flops 151257088 | bytes 1441792 | tf_op jit(solution)/shard_map/kcj,kij->kci/dot_general | solution.py:31
  24.0 0.0 copy-done
  24.0 0.6 %fusion.11 = f32[2,96,256]{2,1,0:T(8,128)S(1)} fusion(f32[2,96,256]{2,1,0:T(8,128)S(1)} %fusion, f32[2,256,256]{2,1,0:T(8,128)S(1)} %copy-done), kind=kOutput, calls=%fused_computation.64 | convolution fusion | flops 150994944 | bytes 917504 | tf_op jit(solution)/shard_map/kcj,kij->kci/dot_general | solution.py:32
  24.6 1.1 %copy.37 = f32[2,96,512]{2,0,1:T(2,128)} copy(f32[2,96,512]{2,1,0:T(8,128)S(1)} %pad_maximum_fusion) | data formatting | bytes 786432 | tf_op jit(solution)/shard_map/concatenate | solution.py:33
  25.7 3.6 %all-to-all-start.1 = ((f32[2,96,512]{2,0,1:T(2,128)}), f32[2,96,512]{2,0,1:T(2,128)S(1)}, u32[]{:S(2)}, u32[]{:S(2)}) async-start(f32[2,96,512]{2,0,1:T(2,128)} %copy.37), calls=%async_computation.1 | async-start | bytes 786432 | tf_op jit(solution)/shard_map/all_to_all | solution.py:53
  29.2 0.1 copy.40
  29.3 0.1 reshape.118
  29.4 11.8 %all-to-all-done.1 = f32[2,96,512]{2,0,1:T(2,128)S(1)} async-done(((f32[2,96,512]{2,0,1:T(2,128)}), f32[2,96,512]{2,0,1:T(2,128)S(1)}, u32[]{:S(2)}, u32[]{:S(2)}) %all-to-all-start.1) | async-done | bytes 393248 | tf_op jit(solution)/shard_map/all_to_all | solution.py:53
  41.3 0.1 copy.42
  41.4 0.6 %gather_fusion.1 = f32[16,6,512]{2,1,0:T(8,128)S(1)} fusion(f32[32,6,512]{2,1,0:T(8,128)S(1)} %bitcast.102, s32[1024]{0:T(1024)S(1)} %get-tuple-element.9), kind=kCustom, calls=%fused_computation.1 | custom fusion | bytes 393280 | tf_op jit(solution)/shard_map/gather | solution.py:54
  42.0 1.5 %scatter_fusion.1 = f32[6,48,128]{2,0,1:T(8,128)S(1)} fusion(f32[6,48,128]{2,0,1:T(8,128)S(1)} %copy_multiply_fusion, s32[32]{0:T(128)S(1)} %fusion.8, f32[32,6,128]{2,1,0:T(8,128)S(1)} %bitcast.106), kind=kCustom, calls=%fused_computation.3 | custom fusion | bytes 295040 | tf_op jit(solution)/shard_map/scatter | solution.py:57
  43.5 1.7 %scatter_fusion.2 = f32[6,48,128]{2,0,1:T(8,128)S(1)} fusion(f32[6,48,128]{2,0,1:T(8,128)S(1)} %scatter_fusion.1, s32[32]{0:T(128)S(1)} %fusion.9, f32[32,6,128]{2,1,0:T(8,128)S(1)} %bitcast.105), kind=kCustom, calls=%fused_computation.4 | custom fusion | flops 24576 | bytes 295040 | tf_op jit(solution)/shard_map/scatter-add | solution.py:58
  45.1 0.8 %copy.41 = f32[1,6,6144]{2,0,1:T(1,128)} copy(f32[1,6,6144]{2,1,0:T(8,128)S(1)} %bitcast.100) | data formatting | bytes 294912 | tf_op jit(solution)/shard_map/broadcast_in_dim;reshape | solution.py:59
  (29 shorter events, 0.2 us)
Async XLA Ops:
  0.0 24.0 %copy-start = (f32[2,256,256]{2,1,0:T(8,128)S(1)}, f32[2,256,256]{2,1,0:T(8,128)}, u32[]{:S(2)}) copy-start(f32[2,256,256]{2,1,0:T(8,128)} %param.11) | copy-start | bytes 1572868
  0.0 0.8 %copy-start.2 = (s32[16,4]{0,1:T(4,128)S(1)}, s32[16,4]{0,1:T(4,128)}, u32[]{:S(2)}) copy-start(s32[16,4]{0,1:T(4,128)} %param.8) | copy-start | bytes 772
  1.0 0.7 %copy-start.3 = (s32[16]{0:T(128)S(1)}, s32[16]{0:T(128)}, u32[]{:S(2)}) copy-start(s32[16]{0:T(128)} %param.9) | copy-start | bytes 196
  1.6 0.7 %copy-start.4 = (s32[48,1]{0,1:T(1,128)S(1)}, s32[48,1]{0,1:T(1,128)}, u32[]{:S(2)}) copy-start(s32[48,1]{0,1:T(1,128)} %param.7) | copy-start | bytes 580
  6.2 17.1 %copy-start.1 = (f32[2,256,256]{2,1,0:T(8,128)S(1)}, f32[2,256,256]{2,1,0:T(8,128)}, u32[]{:S(2)}) copy-start(f32[2,256,256]{2,1,0:T(8,128)} %param.10) | copy-start | bytes 1572868
  6.2 17.1 %all-to-all-start = ((f32[16,2,6,256]{3,1,2,0:T(2,128)}), f32[16,2,6,256]{3,1,2,0:T(2,128)S(1)}, u32[]{:S(2)}, u32[]{:S(2)}) async-start(f32[16,2,6,256]{3,1,2,0:T(2,128)} %copy.35), calls=%async_computation | async-start | bytes 393216 | tf_op jit(solution)/shard_map/all_to_all | solution.py:13
  25.7 15.6 %all-to-all-start.1 = ((f32[2,96,512]{2,0,1:T(2,128)}), f32[2,96,512]{2,0,1:T(2,128)S(1)}, u32[]{:S(2)}, u32[]{:S(2)}) async-start(f32[2,96,512]{2,0,1:T(2,128)} %copy.37), calls=%async_computation.1 | async-start | bytes 786432 | tf_op jit(solution)/shard_map/all_to_all | solution.py:53
